TPU v7x, 32 devices: a whole 2x2x4 slice. The times are simulated.
32 devices in a mesh: dp: 2 (over x), tp2: 4 (over z), tp: 4 (over y, core).
Axes of the slice: x: 2, y: 2, z: 4, core: 2. Of those that a mesh axis runs over, the one named last changes fastest.
Arguments:
- attn_out: bfloat16 [32768, 5120], P('dp', 'tp'), parts along dimension 0
- w_out: bfloat16 [5120, 5120], P('tp', 'tp2')
- residual: bfloat16 [32768, 5120], P(('dp', 'tp'), 'tp2'), parts along dimension 0
- norm_gain: float32 [5120], P('tp2')
Outputs:
- output 1: bfloat16 [32768, 5120], P(('dp', 'tp'), 'tp2'), parts along dimension 0
- output 2: bfloat16 [32768, 5120], P(('dp', 'tp'), 'tp2'), parts along dimension 0
There are 2 independent parts. A program takes and returns all parts, laid end to end along the dimension named above; an argument that names none is the same for every part.
All inputs are finite; a program needn't handle non-finite values.
Results may differ from a plain program's by a relative error of at most 0.00720159.
Values are sent between devices in bfloat16 or wider.
A program may use at most 1 GiB of HBM per device.

v0:
```python
import jax
import jax.numpy as jnp
from jax import lax
from jax.sharding import PartitionSpec as P, NamedSharding

EPS_NORM = 1e-6


def solution(mesh):
    tp_size = mesh.shape["tp"]
    col_groups = mesh.shape["tp2"]

    def local_step(attn_blk, w_blk, res_blk, gain_blk):
        block_prod = jnp.dot(attn_blk, w_blk, preferred_element_type=jnp.float32).astype(jnp.bfloat16)
        token_rows, local_cols = block_prod.shape
        received = lax.all_to_all(block_prod, "tp", 0, 0, tiled=True)
        y_sum = jnp.sum(received.reshape(tp_size, token_rows // tp_size, local_cols), axis=0, dtype=jnp.float32)
        hidden = res_blk.astype(jnp.float32) + y_sum
        sq_sum = lax.psum(jnp.sum(hidden * hidden, axis=-1, keepdims=True), "tp2")
        inv_rms = lax.rsqrt(sq_sum / (local_cols * col_groups) + EPS_NORM)
        normed = hidden * inv_rms * gain_blk
        return hidden.astype(jnp.bfloat16), normed.astype(jnp.bfloat16)

    row_spec = P(("dp", "tp"), "tp2")
    return jax.shard_map(local_step, mesh=mesh, in_specs=(P("dp", "tp"), P("tp", "tp2"), row_spec, P("tp2")), out_specs=(row_spec, row_spec), check_vma=False)
```

profile of v0, /device:TPU:0, one launch (start us, length us, event | category | flops | bytes accessed | tf_op | source)
XLA Modules:
  0.0 618.5 jit_solution(16043135242515290207)
XLA Ops:
  0.6 0.0 copy-start
  0.6 1.9 copy-done
  2.6 62.2 %convolution_convert_fusion = bf16[16384,1280]{1,0:T(8,128)(2,1)} fusion(bf16[16384,1280]{1,0:T(8,128)(2,1)} %param.4, bf16[1280,1280]{1,0:T(8,128)(2,1)S(1)} %copy-done), kind=kOutput, calls=%fused_computation.1 | convolution fusion | flops 53708062720 | bytes 87162880 | tf_op jit(solution)/shard_map/dot_general | solution.py:14
  64.8 0.0 slice-start
  64.8 0.0 slice-start.1
  64.8 475.6 %all_to_all.9 = bf16[4,4096,1280]{2,1,0:T(8,128)(2,1)} all-to-all(bf16[4,4096,1280]{2,1,0:T(8,128)(2,1)} %bitcast.7), channel_id=1, replica_groups=mesh['dp'=2,'tp2'=4,'tp'=4] {'tp'}, dimensions={0} | all-to-all | bytes 83886080 | tf_op jit(solution)/shard_map/all_to_all | solution.py:16
  540.4 0.0 slice-start.2
  540.4 30.2 %convert_reduce_fusion = f32[4096,1280]{1,0:T(8,128)} fusion(bf16[4,4096,1280]{2,1,0:T(8,128)(2,1)} %all_to_all.9), kind=kLoop, calls=%fused_computation | loop fusion | flops 36700160 | bytes 62914560 | tf_op jit(solution)/shard_map/reduce_sum | solution.py:17
  570.6 0.0 slice-done
  570.6 0.0 slice-done.1
  570.6 0.0 slice-done.2
  570.6 0.0 copy-start.2
  570.6 9.0 %multiply_reduce_fusion = f32[4096]{0:T(1024)S(1)} fusion(f32[4096,1280]{1,0:T(8,128)} %convert_reduce_fusion, bf16[4096,1280]{1,0:T(8,128)(2,1)S(1)} %bitcast.6), kind=kLoop, calls=%fused_computation.3 | loop fusion | flops 20967424 | bytes 31473664 | tf_op jit(solution)/shard_map/reduce_sum | solution.py:19
  579.5 19.5 %psum.7 = f32[4096,1]{0,1:T(1,128)S(1)} all-reduce(f32[4096,1]{0,1:T(1,128)S(1)} %bitcast.9), channel_id=1, replica_groups=mesh['dp'=2,'tp2'=4,'tp'=4] {'tp2'}, use_global_device_ids=true, to_apply=%region_2.0 | all-reduce | flops 4096 | bytes 32768 | tf_op jit(solution)/shard_map/psum | solution.py:19
  599.1 0.0 copy-start.1
  599.1 0.0 copy-done.2
  599.1 19.4 %multiply_convert_fusion = (bf16[4096,1280]{1,0:T(8,128)(2,1)}, bf16[4096,1280]{1,0:T(8,128)(2,1)}) fusion(f32[1280]{0:T(1024)S(1)} %copy-done.2, f32[4096]{0:T(1024)S(1)} %bitcast.8, f32[4096,1280]{1,0:T(8,128)} %convert_reduce_fusion, bf16[4096,1280]{1,0:T(8,128)(2,1)} %param.6), kind=kLoop, calls=%fused_computation.2 | loop fusion | flops 31457280 | bytes 52450304 | tf_op jit(solution)/shard_map/convert_element_type | solution.py:22
  618.5 0.0 copy-done.1
  (2 shorter events, 0.0 us)
Async XLA Ops:
  0.6 1.9 copy-start
  64.8 505.8 %slice-start = ((s8[10485760]{0:T(1024)(128)(4,1)}), s8[4194304]{0:T(1024)(128)(4,1)S(1)}, s32[]{:S(2)}) async-start(s8[10485760]{0:T(1024)(128)(4,1)} %bitcast.5), calls=%async_computation.1 | async-start | bytes 8388608
  64.8 505.8 %slice-start.1 = ((s8[10485760]{0:T(1024)(128)(4,1)}), s8[4194304]{0:T(1024)(128)(4,1)S(1)}, s32[]{:S(2)}) async-start(s8[10485760]{0:T(1024)(128)(4,1)} %bitcast.5), calls=%async_computation.2 | async-start | bytes 8388608
  540.4 30.2 %slice-start.2 = ((s8[10485760]{0:T(1024)(128)(4,1)}), s8[2097152]{0:T(1024)(128)(4,1)S(1)}, s32[]{:S(2)}) async-start(s8[10485760]{0:T(1024)(128)(4,1)} %bitcast.5), calls=%async_computation.3 | async-start | bytes 4194304
  570.6 28.5 %copy-start.2 = (f32[1280]{0:T(1024)S(1)}, f32[1280]{0:T(1024)}, u32[]{:S(2)}) copy-start(f32[1280]{0:T(1024)} %param.7) | copy-start | bytes 15364
  599.1 19.4 %copy-start.1 = (bf16[1280,1280]{1,0:T(8,128)(2,1)S(1)}, bf16[1280,1280]{1,0:T(8,128)(2,1)}, u32[]{:S(2)}) copy-start(bf16[1280,1280]{1,0:T(8,128)(2,1)} %param.5) | copy-start | bytes 9830404
where the time goes:
time: 619 us; the launch traced here: 618 us
  blocking collectives  495 us (80%)
  matrix products  62.2 us (10%)
  other arithmetic  58.6 us (9%)
    all_to_all x1, blocking collectives, local_step(): received = lax.all_to_all(block_prod, 'tp', 0, 0, tiled=True)  476 us
    dot_general x1, matrix products, local_step(): jnp.dot(attn_blk, w_blk, preferred_element_type=jnp.float32)  62.2 us
    reduce_sum x1, other arithmetic, local_step(): jnp.sum(received.reshape(tp_size, token_rows // tp_size, local_cols), axi...  30.2 us
    psum x1, blocking collectives, local_step(): sq_sum = lax.psum(jnp.sum(hidden * hidden, axis=-1, keepdims=True), 'tp2')  19.5 us
    convert_element_type x1, other arithmetic, local_step(): return (hidden.astype(jnp.bfloat16), normed.astype(jnp.bfloat16))  19.4 us

commit v1 on v0

v1 whole, which is shorter than its diff:
```python
import functools

import jax
import jax.numpy as jnp
from jax import lax
from jax.experimental import pallas as pl
from jax.experimental.pallas import tpu as pltpu
from jax.sharding import PartitionSpec as P

EPS_NORM = 1e-6
MESH = pl.DeviceIdType.MESH
F32, BF16 = jnp.float32, jnp.bfloat16

NCH, NU, NY, NE = 64, 30, 30, 4
NV = NCH - NU
LOOK = 3
TILE = 128
LOCAL = 256


def gather_matmul(a, w, res, h, ss_out, asib, arem, wbuf, abuf, sbuf, rbuf, ss_own, ss_all,
                  ld, own_w, sib_recv, sib_send, y_recv, y_send, z_recv, z_send, e_recv, e_send, w_recv, w_send, ss_recv, ss_send):
    x, z, t = lax.axis_index("dp"), lax.axis_index("tp2"), lax.axis_index("tp")
    rows, width = h.shape
    depth = w.shape[0]
    half = depth // 2
    ch = rows // NCH
    core, yy = lax.rem(t, 2), t // 2
    sib = yy * 2 + 1 - core
    far = (1 - yy) * 2
    zp = z + 1 - 2 * lax.rem(z, 2)
    middle = lax.rem((z + 1) // 2, 2)
    n_local = rows // LOCAL

    def aligned(v, m=ch):
        return pl.multiple_of(v, m)

    def y_row(zz, k):
        mid = lax.rem((zz + 1) // 2, 2)
        early = 1 - jnp.minimum(k // NE, 1)
        return (mid * NU + k + mid * lax.rem(zz, 2) * early * (NV - NE)) * ch

    def e_row(j):
        return (NU + (z // 2) * (NV - NE) + j) * ch

    def y_send_to(k, r):
        row = y_row(z, k)
        return pltpu.make_async_remote_copy(
            src_ref=a.at[pl.ds(aligned((far + r) * rows + row), ch)], dst_ref=arem.at[pl.ds(aligned(core * rows + row), ch)],
            send_sem=y_send, recv_sem=y_recv.at[core, k], device_id=(x, z, far + r), device_id_type=MESH)

    def start_y(k):
        for r in range(2):
            y_send_to(k, r).start()

    def move(row, s, recv, k, send, dev):
        ref = arem.at[pl.ds(aligned(s * rows + row), ch)]
        return pltpu.make_async_remote_copy(src_ref=ref, dst_ref=ref, send_sem=send, recv_sem=recv.at[s, k], device_id=dev, device_id_type=MESH)

    def each(row, recv, k, send, dev, start):
        for s in range(2):
            c = move(row, s, recv, k, send, dev)
            c.start() if start else c.wait_recv()

    def wait_y(k):
        each(y_row(z, k), y_recv, k, z_send, (x, zp, t), False)

    def relay_z(k):
        each(y_row(z, k), z_recv, k, z_send, (x, zp, t), True)

    def wait_z(k):
        each(y_row(zp, k), z_recv, k, z_send, (x, zp, t), False)

    def w_move(slot, part, idx, dev, src=None):
        ref = wbuf.at[pl.ds(aligned(slot * depth + part * half, 128), half)]
        return pltpu.make_async_remote_copy(src_ref=ref if src is None else src, dst_ref=ref, send_sem=w_send.at[idx], recv_sem=w_recv.at[idx],
                                            device_id=dev, device_id_type=MESH)

    w_sib = pltpu.make_async_remote_copy(src_ref=w, dst_ref=wbuf.at[pl.ds(depth, depth)], send_sem=w_send.at[0], recv_sem=w_recv.at[0],
                                         device_id=(x, z, sib), device_id_type=MESH)
    w_y = w_move(2 + core, x, 1, (x, z, far + core), w.at[pl.ds(aligned(x * half, 128), half)])
    w_x = w_move(2 + core, x, 2, (1 - x, z, t))
    w_x_in = w_move(2 + core, 1 - x, 2, (1 - x, z, t))
    w_d0 = w_move(2 + core, x, 3, (x, z, sib))
    w_d1 = w_move(2 + core, 1 - x, 4, (x, z, sib))
    w_d0_in = w_move(3 - core, x, 3, (x, z, sib))
    w_d1_in = w_move(3 - core, 1 - x, 4, (x, z, sib))

    def sib_copy(i):
        return pltpu.make_async_remote_copy(
            src_ref=a.at[pl.ds(aligned(sib * rows + i * LOCAL), LOCAL)], dst_ref=asib.at[pl.ds(aligned(i * LOCAL), LOCAL)],
            send_sem=sib_send, recv_sem=sib_recv.at[i], device_id=(x, z, sib), device_id_type=MESH)

    def loads(i):
        slot = lax.rem(i, 2)
        here = pl.ds(aligned(i * LOCAL), LOCAL)
        return (pltpu.make_async_copy(a.at[pl.ds(aligned(t * rows + i * LOCAL), LOCAL)], abuf.at[slot], ld.at[slot, 0]),
                pltpu.make_async_copy(asib.at[here], sbuf.at[slot], ld.at[slot, 1]),
                pltpu.make_async_copy(res.at[here], rbuf.at[slot], ld.at[slot, 2]))

    def prefetch(i):
        sib_copy(i).wait_recv()
        for c in loads(i):
            c.start()

    def block(lhs, slot, cols):
        return jnp.dot(lhs, wbuf[pl.ds(slot * depth, depth), cols], preferred_element_type=F32).astype(BF16).astype(F32)

    def local_tile(i):
        slot = lax.rem(i, 2)
        for c in loads(i):
            c.wait()

        @pl.when(i + 1 < n_local)
        def _():
            prefetch(i + 1)

        here = pl.ds(aligned(i * LOCAL), LOCAL)
        for n in range(width // 256):
            cols = pl.ds(n * 256, 256)
            h[here, cols] = rbuf[slot, :, cols].astype(F32) + block(abuf[slot], 0, cols) + block(sbuf[slot], 1, cols)

    def remote_tile(row):
        acc = jnp.zeros((TILE, 128), F32)
        here = pl.ds(aligned(row, TILE), TILE)
        there = pl.ds(aligned(rows + row, TILE), TILE)
        for n in range(width // 256):
            cols = pl.ds(n * 256, 256)
            v = h[here, cols] + block(arem[here, :], 2, cols) + block(arem[there, :], 3, cols)
            h[here, cols] = v
            sq = v * v
            acc = acc + sq[:, :128] + sq[:, 128:]
        ss_own[pl.ds(row // TILE, 1), :] = jnp.sum(acc.T, axis=0, keepdims=True)

    def pair(i):
        wait_z(2 * i)
        wait_z(2 * i + 1)

        def one(q, c):
            remote_tile(y_row(z + q * (zp - z), 2 * i))
            return c

        lax.fori_loop(0, 2, one, 0)

    for k in range(LOOK):
        start_y(k)
    own = pltpu.make_async_copy(w, wbuf.at[pl.ds(0, depth)], own_w)
    own.start()
    w_sib.start()
    lax.fori_loop(0, n_local, lambda i, c: (sib_copy(i).start(), c)[1], 0)
    prefetch(0)
    own.wait()
    w_sib.wait_recv()

    def first(k, c):
        wait_y(k)
        relay_z(k)

        @pl.when(middle == 1)
        def _():
            each(y_row(z, k), e_recv, k, e_send, (x, 3 - z, t), True)

        start_y(k + LOOK)

        @pl.when(k == 0)
        def _():
            w_y.start()

        local_tile(k)
        return c

    lax.fori_loop(0, NE, first, 0)

    def extra(j, c):
        local_tile(NE + 2 * j)
        each(e_row(j), e_recv, j, e_send, (x, zp, t), False)

        @pl.when(middle == 1)
        def _():
            each(e_row(j), e_recv, j, e_send, (x, zp, t), True)

        local_tile(NE + 2 * j + 1)
        return c

    lax.fori_loop(0, NE, extra, 0)
    w_y.wait_recv()
    w_x.start()
    w_d0.start()

    def second(k, c):
        wait_y(k)
        relay_z(k)
        start_y(k + LOOK)

        @pl.when(k < NE + 4)
        def _():
            local_tile(3 * NE + k - NE)

        return c

    lax.fori_loop(NE, 10, second, 0)
    w_x_in.wait_recv()
    w_d1.start()
    w_d0_in.wait_recv()
    w_d1_in.wait_recv()

    def step(k):
        wait_y(k)
        relay_z(k)

        @pl.when(k + LOOK < NY)
        def _():
            start_y(k + LOOK)

    def third(k, c):
        step(k)

        @pl.when(k == 10)
        def _():
            lax.fori_loop(0, 2, lambda j, d: (remote_tile(e_row(2 * j)), d)[1], 0)

        pair(k - 10)
        return c

    lax.fori_loop(10, 19, third, 0)

    def fourth(i, c):
        step(2 * i + 1)

        @pl.when(i < NY // 2 - 1)
        def _():
            step(2 * i + 2)

        pair(i)
        return c

    lax.fori_loop(9, NY // 2, fourth, 0)

    sends = []
    for d in range(1, 4):
        zz = lax.rem(z + d, 4)
        c = pltpu.make_async_remote_copy(src_ref=ss_own, dst_ref=ss_all.at[z], send_sem=ss_send.at[d], recv_sem=ss_recv.at[z],
                                         device_id=(x, zz, t), device_id_type=MESH)
        c.start()
        sends.append(c)
    y_total = 2 * NY * ch
    pltpu.make_async_remote_copy(src_ref=a.at[pl.ds(0, y_total)], dst_ref=arem.at[pl.ds(0, y_total)], send_sem=y_send, recv_sem=y_recv.at[0, 0],
                                 device_id=(x, z, far), device_id_type=MESH).wait_send()
    pltpu.make_async_remote_copy(src_ref=arem.at[pl.ds(0, y_total)], dst_ref=arem.at[pl.ds(0, y_total)], send_sem=z_send, recv_sem=z_recv.at[0, 0],
                                 device_id=(x, zp, t), device_id_type=MESH).wait_send()

    @pl.when(middle == 1)
    def _():
        n = 4 * NE * ch
        pltpu.make_async_remote_copy(src_ref=arem.at[pl.ds(0, n)], dst_ref=arem.at[pl.ds(0, n)], send_sem=e_send, recv_sem=e_recv.at[0, 0],
                                     device_id=(x, zp, t), device_id_type=MESH).wait_send()

    pltpu.make_async_remote_copy(src_ref=a.at[pl.ds(0, rows)], dst_ref=asib, send_sem=sib_send, recv_sem=sib_recv.at[0],
                                 device_id=(x, z, sib), device_id_type=MESH).wait_send()
    for c in (w_sib, w_y, w_x, w_d0, w_d1):
        c.wait_send()
    total = ss_own[...]
    for d in range(1, 4):
        zz = lax.rem(z + d, 4)
        pltpu.make_async_remote_copy(src_ref=ss_own, dst_ref=ss_all.at[zz], send_sem=ss_send.at[d], recv_sem=ss_recv.at[zz],
                                     device_id=(x, zz, t), device_id_type=MESH).wait_recv()
    ss_all[pl.ds(z, 1)] = total[None]
    ss_out[...] = (ss_all[0] + ss_all[1]) + (ss_all[2] + ss_all[3])
    for c in sends:
        c.wait_send()


def normalize(total_cols, h, ss, gain, h_out, n_out):
    i = pl.program_id(0)
    rows = h_out.shape[0]
    for b in range(rows // TILE):
        at = pl.multiple_of(i * rows + b * TILE, TILE)
        inv = lax.rsqrt(ss[pl.ds(i * (rows // TILE) + b, 1), :] / total_cols + EPS_NORM)
        inv = jnp.broadcast_to(inv, (TILE, TILE)).T
        here = pl.ds(b * TILE, TILE)
        for c in range(h_out.shape[1] // 128):
            cols = pl.ds(c * 128, 128)
            v = h[pl.ds(at, TILE), cols]
            h_out[here, cols] = v.astype(BF16)
            n_out[here, cols] = (v * inv * gain[:, cols]).astype(BF16)


def solution(mesh):
    col_groups = mesh.shape["tp2"]
    n_tp = mesh.shape["tp"]

    def local_step(a, w, res, gain):
        rows, width = res.shape
        depth = w.shape[0]
        dma = pltpu.SemaphoreType.DMA
        h, ss, _ = pl.pallas_call(
            gather_matmul,
            out_shape=(pltpu.VMEM((rows, width), F32), pltpu.VMEM((rows // TILE, 128), F32),
                       jax.ShapeDtypeStruct((rows, depth), BF16)),
            in_specs=[pl.BlockSpec(memory_space=pl.ANY)] * 3,
            out_specs=(pl.BlockSpec(memory_space=pltpu.VMEM), pl.BlockSpec(memory_space=pltpu.VMEM), pl.BlockSpec(memory_space=pl.ANY)),
            scratch_shapes=[
                pltpu.VMEM((2 * rows, depth), BF16), pltpu.VMEM((n_tp * depth, width), BF16),
                pltpu.VMEM((2, LOCAL, depth), BF16), pltpu.VMEM((2, LOCAL, depth), BF16), pltpu.VMEM((2, LOCAL, width), BF16),
                pltpu.VMEM((rows // TILE, 128), F32), pltpu.VMEM((4, rows // TILE, 128), F32),
                dma((2, 3)), dma, dma((rows // LOCAL,)), dma, dma((2, NY)), dma, dma((2, NY)), dma, dma((2, NE)), dma,
                dma((5,)), dma((5,)), dma((4,)), dma((4,)),
            ],
            compiler_params=pltpu.CompilerParams(has_side_effects=True, vmem_limit_bytes=42 * 1024 * 1024),
            cost_estimate=pl.CostEstimate(flops=2 * rows * n_tp * depth * width, bytes_accessed=8 * rows * width, transcendentals=0),
            name="gather_matmul",
        )(a, w, res)
        blk = 512
        return pl.pallas_call(
            functools.partial(normalize, width * col_groups),
            grid=(rows // blk,),
            out_shape=(jax.ShapeDtypeStruct((rows, width), BF16),) * 2,
            in_specs=[pl.BlockSpec(memory_space=pltpu.VMEM)] * 3,
            out_specs=(pl.BlockSpec((blk, width), lambda i: (i, 0)),) * 2,
            compiler_params=pltpu.CompilerParams(vmem_limit_bytes=16 * 1024 * 1024),
            name="normalize",
        )(h, ss, gain.reshape(1, width))

    row_spec = P(("dp", "tp"), "tp2")
    return jax.shard_map(local_step, mesh=mesh, in_specs=(P("dp", "tp"), P("tp", "tp2"), row_spec, P("tp2")), out_specs=(row_spec, row_spec), check_vma=False)
```

time: 619 us -> 280 us (0.45)
  blocking collectives: 495 us -> 0 us
  Pallas kernels: 0 us -> 277 us
  matrix products: 62.2 us -> 0 us
  other arithmetic: 58.6 us -> 0 us
    all_to_all x1 -> x0, blocking collectives: 476 us -> none  [local_step(): received = lax.all_to_all(block_prod, 'tp', 0, 0, tiled=True)]
    pallas_call x0 -> x2, Pallas kernels: none -> 277 us  [the longest x1 269 us: local_step(): pl.pallas_call(gather_matmul, out_shape=(pltpu.VMEM((rows, width), F32),...]
    dot_general x1 -> x0, matrix products: 62.2 us -> none  [local_step(): jnp.dot(attn_blk, w_blk, preferred_element_type=jnp.float32)]
    reduce_sum x2 -> x0, other arithmetic: 39.2 us -> none  [the longest x1 30.2 us: local_step(): jnp.sum(received.reshape(tp_size, token_rows // tp_size, local_cols), axi...]
    psum x1 -> x0, blocking collectives: 19.5 us -> none  [local_step(): sq_sum = lax.psum(jnp.sum(hidden * hidden, axis=-1, keepdims=True), 'tp2')]
    convert_element_type x1 -> x0, other arithmetic: 19.4 us -> none  [local_step(): return (hidden.astype(jnp.bfloat16), normed.astype(jnp.bfloat16))]
where the time goes in v1:
time: 280 us; the launch traced here: 279 us
  Pallas kernels  277 us (99%)
    pallas_call x1, Pallas kernels, local_step(): pl.pallas_call(gather_matmul, out_shape=(pltpu.VMEM((rows, width), F32),...  269 us
    pallas_call x1, Pallas kernels, local_step(): pl.pallas_call(functools.partial(normalize, width * col_groups), grid=(ro...  8.54 us

profile of v1, /device:TPU:0, one launch (start us, length us, event | category | flops | bytes accessed | tf_op | source)
XLA Modules:
  0.0 278.6 jit_solution(12287228621146341950)
XLA Ops:
  0.6 0.7 reshape.7.gain
  1.3 268.7 %gather_matmul.1 = (f32[4096,1280]{1,0:T(8,128)S(1)}, f32[32,128]{1,0:T(8,128)S(1)}, bf16[4096,1280]{1,0:T(8,128)(2,1)}) custom-call(bf16[16384,1280]{1,0:T(8,128)(2,1)} %a.1, bf16[1280,1280]{1,0:T(8,128)(2,1)} %w.1, bf16[4096,1280]{1,0:T(8,128)(2,1)} %res.1), custom_call_target="tpu_custom_call" | custom-call | flops 53687091200 | bytes 41943040 | tf_op jit(solution)/shard_map/gather_matmul/pallas_call | solution.py:296
  270.0 8.5 %normalize.1 = (bf16[4096,1280]{1,0:T(8,128)(2,1)}, bf16[4096,1280]{1,0:T(8,128)(2,1)}) custom-call(f32[4096,1280]{1,0:T(8,128)S(1)} %get-tuple-element.4.h, f32[32,128]{1,0:T(8,128)S(1)} %get-tuple-element.5.ss, f32[1,1280]{1,0:T(1,128)S(1)} %reshape.7.gain), custom_call_target="tpu_custom_call" | custom-call | tf_op jit(solution)/shard_map/normalize/pallas_call | solution.py:314

commit v2 on v1

--- a/solution.py
+++ b/solution.py
@@ -11,15 +11,16 @@
 MESH = pl.DeviceIdType.MESH
 F32, BF16 = jnp.float32, jnp.bfloat16
 
-NCH, NU, NY, NE = 64, 30, 30, 4
-NV = NCH - NU
-LOOK = 3
+NCH, NU, NY, NR, NE = 128, 60, 60, 56, 12
+LOOK = 6
+CATCH, CAUGHT = 24, 10
 TILE = 128
 LOCAL = 256
+STORE = 128
 
 
 def gather_matmul(a, w, res, h, ss_out, asib, arem, wbuf, abuf, sbuf, rbuf, ss_own, ss_all,
-                  ld, own_w, sib_recv, sib_send, y_recv, y_send, z_recv, z_send, e_recv, e_send, w_recv, w_send, ss_recv, ss_send):
+                  ss_last, ss_lasts, ld, own_w, sib_recv, sib_send, y_recv, y_send, z_recv, z_send, e_recv, e_send, w_recv, w_send, ss_recv, ss_send, sl_recv, sl_send):
     x, z, t = lax.axis_index("dp"), lax.axis_index("tp2"), lax.axis_index("tp")
     rows, width = h.shape
     depth = w.shape[0]
@@ -38,10 +39,11 @@
     def y_row(zz, k):
         mid = lax.rem((zz + 1) // 2, 2)
         early = 1 - jnp.minimum(k // NE, 1)
-        return (mid * NU + k + mid * lax.rem(zz, 2) * early * (NV - NE)) * ch
+        late = jnp.minimum(k // NR, 1)
+        return (k + mid * (1 - late) * NU + mid * lax.rem(zz, 2) * early * NR) * ch
 
     def e_row(j):
-        return (NU + (z // 2) * (NV - NE) + j) * ch
+        return (NU + (z // 2) * NR + j) * ch
 
     def y_send_to(k, r):
         row = y_row(z, k)
@@ -130,17 +132,26 @@
             h[here, cols] = v
             sq = v * v
             acc = acc + sq[:, :128] + sq[:, 128:]
-        ss_own[pl.ds(row // TILE, 1), :] = jnp.sum(acc.T, axis=0, keepdims=True)
-
-    def pair(i):
-        wait_z(2 * i)
-        wait_z(2 * i + 1)
-
-        def one(q, c):
-            remote_tile(y_row(z + q * (zp - z), 2 * i))
-            return c
-
-        lax.fori_loop(0, 2, one, 0)
+        return jnp.sum(acc.T, axis=0, keepdims=True)
+
+    def tile(row):
+        ss_own[pl.ds(row // TILE, 1), :] = remote_tile(row)
+
+    cpt = TILE // ch
+
+    def y_tile(i):
+        tile(y_row(z, cpt * i))
+
+    def z_tile(i):
+        for s in range(cpt):
+            wait_z(cpt * i + s)
+        tile(y_row(zp, cpt * i))
+
+    barrier = pltpu.get_barrier_semaphore()
+    partners = [(x, z, far), (x, z, far + 1), (x, z, sib), (1 - x, z, t)] + [(x, lax.rem(z + d, 4), t) for d in range(1, 4)]
+    for dev in partners:
+        pl.semaphore_signal(barrier, inc=1, device_id=dev, device_id_type=MESH)
+    pl.semaphore_wait(barrier, len(partners))
 
     for k in range(LOOK):
         start_y(k)
@@ -152,101 +163,107 @@
     own.wait()
     w_sib.wait_recv()
 
+    def step(k):
+        wait_y(k)
+
+        @pl.when(k < NR)
+        def _():
+            relay_z(k)
+
+        @pl.when(k + LOOK < NY)
+        def _():
+            start_y(k + LOOK)
+
     def first(k, c):
-        wait_y(k)
-        relay_z(k)
+        step(k)
 
         @pl.when(middle == 1)
         def _():
             each(y_row(z, k), e_recv, k, e_send, (x, 3 - z, t), True)
 
-        start_y(k + LOOK)
-
-        @pl.when(k == 0)
+        @pl.when(k == NE - 1 - LOOK)
         def _():
             w_y.start()
 
-        local_tile(k)
+        @pl.when(lax.rem(k, 2) == 1)
+        def _():
+            local_tile(k // 2)
+
         return c
 
     lax.fori_loop(0, NE, first, 0)
 
     def extra(j, c):
-        local_tile(NE + 2 * j)
         each(e_row(j), e_recv, j, e_send, (x, zp, t), False)
 
         @pl.when(middle == 1)
         def _():
             each(e_row(j), e_recv, j, e_send, (x, zp, t), True)
 
-        local_tile(NE + 2 * j + 1)
+        @pl.when(NE // 2 + j < n_local)
+        def _():
+            local_tile(NE // 2 + j)
+
         return c
 
     lax.fori_loop(0, NE, extra, 0)
     w_y.wait_recv()
     w_x.start()
     w_d0.start()
-
-    def second(k, c):
-        wait_y(k)
-        relay_z(k)
-        start_y(k + LOOK)
-
-        @pl.when(k < NE + 4)
-        def _():
-            local_tile(3 * NE + k - NE)
-
-        return c
-
-    lax.fori_loop(NE, 10, second, 0)
+    lax.fori_loop(NE, CATCH, lambda k, c: (step(k), c)[1], 0)
     w_x_in.wait_recv()
     w_d1.start()
     w_d0_in.wait_recv()
     w_d1_in.wait_recv()
 
-    def step(k):
-        wait_y(k)
-        relay_z(k)
-
-        @pl.when(k + LOOK < NY)
-        def _():
-            start_y(k + LOOK)
-
-    def third(k, c):
-        step(k)
-
-        @pl.when(k == 10)
-        def _():
-            lax.fori_loop(0, 2, lambda j, d: (remote_tile(e_row(2 * j)), d)[1], 0)
-
-        pair(k - 10)
+    def third(i, c):
+        step(CATCH + 2 * i)
+
+        @pl.when(i == 0)
+        def _():
+            lax.fori_loop(0, NE // cpt, lambda j, d: (tile(e_row(cpt * j)), d)[1], 0)
+
+        y_tile(i)
+        step(CATCH + 2 * i + 1)
+        z_tile(i)
         return c
 
-    lax.fori_loop(10, 19, third, 0)
+    lax.fori_loop(0, CAUGHT, third, 0)
+
+    def steps(lo, hi):
+        lax.fori_loop(jnp.maximum(lo, CATCH + 2 * CAUGHT), jnp.minimum(hi, NY), lambda k, c: (step(k), c)[1], 0)
 
     def fourth(i, c):
-        step(2 * i + 1)
-
-        @pl.when(i < NY // 2 - 1)
-        def _():
-            step(2 * i + 2)
-
-        pair(i)
+        steps(cpt * i + 1, cpt * i + cpt)
+        y_tile(i)
+        steps(cpt * i + cpt, cpt * i + cpt + 1)
+        z_tile(i)
         return c
 
-    lax.fori_loop(9, NY // 2, fourth, 0)
-
-    sends = []
-    for d in range(1, 4):
-        zz = lax.rem(z + d, 4)
-        c = pltpu.make_async_remote_copy(src_ref=ss_own, dst_ref=ss_all.at[z], send_sem=ss_send.at[d], recv_sem=ss_recv.at[z],
-                                         device_id=(x, zz, t), device_id_type=MESH)
-        c.start()
-        sends.append(c)
+    lax.fori_loop(CAUGHT, NR // cpt, fourth, 0)
+    steps(NR + 1, NY)
+
+    def share(src, dst, send, recv):
+        for d in range(1, 4):
+            pltpu.make_async_remote_copy(src_ref=src, dst_ref=dst.at[z], send_sem=send.at[d], recv_sem=recv.at[z],
+                                         device_id=(x, lax.rem(z + d, 4), t), device_id_type=MESH).start()
+
+    def collect(src, dst, send, recv):
+        for d in range(1, 4):
+            zz = lax.rem(z + d, 4)
+            pltpu.make_async_remote_copy(src_ref=src, dst_ref=dst.at[zz], send_sem=send.at[d], recv_sem=recv.at[zz],
+                                         device_id=(x, zz, t), device_id_type=MESH).wait()
+        dst[pl.ds(z, 1)] = src[...][None]
+        return (dst[0] + dst[1]) + (dst[2] + dst[3])
+
+    share(ss_own, ss_all, ss_send, ss_recv)
+    ss_last[...] = jnp.broadcast_to(remote_tile(NR * ch), ss_last.shape)
+    share(ss_last, ss_lasts, sl_send, sl_recv)
     y_total = 2 * NY * ch
     pltpu.make_async_remote_copy(src_ref=a.at[pl.ds(0, y_total)], dst_ref=arem.at[pl.ds(0, y_total)], send_sem=y_send, recv_sem=y_recv.at[0, 0],
                                  device_id=(x, z, far), device_id_type=MESH).wait_send()
-    pltpu.make_async_remote_copy(src_ref=arem.at[pl.ds(0, y_total)], dst_ref=arem.at[pl.ds(0, y_total)], send_sem=z_send, recv_sem=z_recv.at[0, 0],
+    z_total = 2 * NR * ch
+    pltpu.make_async_remote_copy(src_ref=arem.at[pl.ds(0, z_total)], dst_ref=arem.at[pl.ds(0, z_total)], send_sem=z_send, recv_sem=z_recv.at[0, 0],
                                  device_id=(x, zp, t), device_id_type=MESH).wait_send()
 
     @pl.when(middle == 1)
@@ -259,30 +276,52 @@
                                  device_id=(x, z, sib), device_id_type=MESH).wait_send()
     for c in (w_sib, w_y, w_x, w_d0, w_d1):
         c.wait_send()
-    total = ss_own[...]
-    for d in range(1, 4):
-        zz = lax.rem(z + d, 4)
-        pltpu.make_async_remote_copy(src_ref=ss_own, dst_ref=ss_all.at[zz], send_sem=ss_send.at[d], recv_sem=ss_recv.at[zz],
-                                     device_id=(x, zz, t), device_id_type=MESH).wait_recv()
-    ss_all[pl.ds(z, 1)] = total[None]
-    ss_out[...] = (ss_all[0] + ss_all[1]) + (ss_all[2] + ss_all[3])
-    for c in sends:
-        c.wait_send()
-
-
-def normalize(total_cols, h, ss, gain, h_out, n_out):
-    i = pl.program_id(0)
-    rows = h_out.shape[0]
-    for b in range(rows // TILE):
-        at = pl.multiple_of(i * rows + b * TILE, TILE)
-        inv = lax.rsqrt(ss[pl.ds(i * (rows // TILE) + b, 1), :] / total_cols + EPS_NORM)
-        inv = jnp.broadcast_to(inv, (TILE, TILE)).T
-        here = pl.ds(b * TILE, TILE)
-        for c in range(h_out.shape[1] // 128):
-            cols = pl.ds(c * 128, 128)
-            v = h[pl.ds(at, TILE), cols]
-            h_out[here, cols] = v.astype(BF16)
-            n_out[here, cols] = (v * inv * gain[:, cols]).astype(BF16)
+    ss_out[...] = collect(ss_own, ss_all, ss_send, ss_recv)
+    ss_out[pl.ds(NR * ch // TILE, 1), :] = collect(ss_last, ss_lasts, sl_send, sl_recv)[:1]
+
+
+def normalize(total_cols, h, ss, gain, h_hbm, n_hbm, h_out, n_out, sem):
+    n_blocks = h.shape[0] // STORE
+
+    def out(i):
+        here = pl.ds(pl.multiple_of(i * STORE, STORE), STORE)
+        buf = pl.ds(pl.multiple_of(lax.rem(i, n_blocks // 2) * STORE, STORE), STORE)
+        return (pltpu.make_async_copy(h_out.at[buf], h_hbm.at[here], sem.at[0, i]),
+                pltpu.make_async_copy(n_out.at[buf], n_hbm.at[here], sem.at[1, i]))
+
+    def start(i):
+        for c in out(i):
+            c.start()
+
+    def wait(i):
+        for c in out(i):
+            c.wait()
+
+    def block(i, carry):
+        @pl.when(i >= n_blocks // 2)
+        def _():
+            wait(i - n_blocks // 2)
+
+        for b in range(STORE // TILE):
+            here = pl.ds(pl.multiple_of(i * STORE + b * TILE, TILE), TILE)
+            to = pl.ds(pl.multiple_of(lax.rem(i, n_blocks // 2) * STORE + b * TILE, TILE), TILE)
+            inv = lax.rsqrt(ss[pl.ds(i * (STORE // TILE) + b, 1), :] / total_cols + EPS_NORM)
+            inv = jnp.broadcast_to(inv, (TILE, TILE)).T
+            for c in range(h.shape[1] // 128):
+                cols = pl.ds(c * 128, 128)
+                v = h[here, cols]
+                h_out[to, cols] = v.astype(BF16)
+                n_out[to, cols] = (v * inv * gain[cols][None, :]).astype(BF16)
+
+        @pl.when(i > 0)
+        def _():
+            start(i - 1)
+
+        return carry
+
+    lax.fori_loop(0, n_blocks, block, 0)
+    start(n_blocks - 1)
+    lax.fori_loop(n_blocks // 2, n_blocks, lambda i, c: (wait(i), c)[1], 0)
 
 
 def solution(mesh):
@@ -302,24 +341,23 @@
             scratch_shapes=[
                 pltpu.VMEM((2 * rows, depth), BF16), pltpu.VMEM((n_tp * depth, width), BF16),
                 pltpu.VMEM((2, LOCAL, depth), BF16), pltpu.VMEM((2, LOCAL, depth), BF16), pltpu.VMEM((2, LOCAL, width), BF16),
-                pltpu.VMEM((rows // TILE, 128), F32), pltpu.VMEM((4, rows // TILE, 128), F32),
+                pltpu.VMEM((rows // TILE, 128), F32), pltpu.VMEM((4, rows // TILE, 128), F32), pltpu.VMEM((8, 128), F32), pltpu.VMEM((4, 8, 128), F32),
                 dma((2, 3)), dma, dma((rows // LOCAL,)), dma, dma((2, NY)), dma, dma((2, NY)), dma, dma((2, NE)), dma,
-                dma((5,)), dma((5,)), dma((4,)), dma((4,)),
+                dma((5,)), dma((5,)), dma((4,)), dma((4,)), dma((4,)), dma((4,)),
             ],
-            compiler_params=pltpu.CompilerParams(has_side_effects=True, vmem_limit_bytes=42 * 1024 * 1024),
+            compiler_params=pltpu.CompilerParams(collective_id=0, has_side_effects=True, vmem_limit_bytes=42 * 1024 * 1024),
             cost_estimate=pl.CostEstimate(flops=2 * rows * n_tp * depth * width, bytes_accessed=8 * rows * width, transcendentals=0),
             name="gather_matmul",
         )(a, w, res)
-        blk = 512
         return pl.pallas_call(
             functools.partial(normalize, width * col_groups),
-            grid=(rows // blk,),
             out_shape=(jax.ShapeDtypeStruct((rows, width), BF16),) * 2,
             in_specs=[pl.BlockSpec(memory_space=pltpu.VMEM)] * 3,
-            out_specs=(pl.BlockSpec((blk, width), lambda i: (i, 0)),) * 2,
-            compiler_params=pltpu.CompilerParams(vmem_limit_bytes=16 * 1024 * 1024),
+            out_specs=(pl.BlockSpec(memory_space=pl.ANY),) * 2,
+            scratch_shapes=[pltpu.VMEM((rows // 2, width), BF16), pltpu.VMEM((rows // 2, width), BF16), dma((2, rows // STORE))],
+            compiler_params=pltpu.CompilerParams(vmem_limit_bytes=14 * 1024 * 1024),
             name="normalize",
-        )(h, ss, gain.reshape(1, width))
+        )(h, ss, gain)
 
     row_spec = P(("dp", "tp"), "tp2")
     return jax.shard_map(local_step, mesh=mesh, in_specs=(P("dp", "tp"), P("tp", "tp2"), row_spec, P("tp2")), out_specs=(row_spec, row_spec), check_vma=False)

time: 280 us -> 271 us (0.968)
  Pallas kernels: 277 us -> 270 us
    pallas_call x1, Pallas kernels: 269 us -> 262 us  [local_step(): pl.pallas_call(gather_matmul, out_shape=(pltpu.VMEM((rows, width), F32),...]
where the time goes in v2:
time: 271 us; the launch traced here: 270 us
  Pallas kernels  270 us (100%)
    pallas_call x1, Pallas kernels, local_step(): pl.pallas_call(gather_matmul, out_shape=(pltpu.VMEM((rows, width), F32),...  262 us
    pallas_call x1, Pallas kernels, local_step(): pl.pallas_call(functools.partial(normalize, width * col_groups), out_shap...  7.82 us

profile of v2, /device:TPU:0, one launch (start us, length us, event | category | flops | bytes accessed | tf_op | source)
XLA Modules:
  0.0 270.5 jit_solution(11248857642629991367)
XLA Ops:
  0.6 0.0 copy-start
  0.6 262.0 %gather_matmul.1 = (f32[4096,1280]{1,0:T(8,128)S(1)}, f32[32,128]{1,0:T(8,128)S(1)}, bf16[4096,1280]{1,0:T(8,128)(2,1)}) custom-call(bf16[16384,1280]{1,0:T(8,128)(2,1)} %a.1, bf16[1280,1280]{1,0:T(8,128)(2,1)} %w.1, bf16[4096,1280]{1,0:T(8,128)(2,1)} %res.1), custom_call_target="tpu_custom_call" | custom-call | flops 53687091200 | bytes 41943040 | tf_op jit(solution)/shard_map/gather_matmul/pallas_call | solution.py:335
  262.7 0.0 copy-done
  262.7 7.8 %normalize.1 = (bf16[4096,1280]{1,0:T(8,128)(2,1)}, bf16[4096,1280]{1,0:T(8,128)(2,1)}) custom-call(f32[4096,1280]{1,0:T(8,128)S(1)} %get-tuple-element.4.h, f32[32,128]{1,0:T(8,128)S(1)} %get-tuple-element.5.ss, f32[1280]{0:T(1024)S(1)} %copy-done), custom_call_target="tpu_custom_call" | custom-call | tf_op jit(solution)/shard_map/normalize/pallas_call | solution.py:352
Async XLA Ops:
  0.6 262.0 %copy-start = (f32[1280]{0:T(1024)S(1)}, f32[1280]{0:T(1024)}, u32[]{:S(2)}) copy-start(f32[1280]{0:T(1024)} %gain.1) | copy-start | bytes 15364

commit v3 on v2

--- a/solution.py
+++ b/solution.py
@@ -11,9 +11,10 @@
 MESH = pl.DeviceIdType.MESH
 F32, BF16 = jnp.float32, jnp.bfloat16
 
-NCH, NU, NY, NR, NE = 128, 60, 60, 56, 12
-LOOK = 6
-CATCH, CAUGHT = 24, 10
+SPLIT = 1
+NCH, NU, NY, NR, NE = 128 * SPLIT, 60 * SPLIT, 60 * SPLIT, 56 * SPLIT, 12 * SPLIT
+LOOK, LAG = 6 * SPLIT, 3
+CATCH, CAUGHT = 24 * SPLIT, 10
 TILE = 128
 LOCAL = 256
 STORE = 128
@@ -185,28 +186,26 @@
         def _():
             w_y.start()
 
-        @pl.when(lax.rem(k, 2) == 1)
-        def _():
-            local_tile(k // 2)
+        @pl.when((middle == 1) & (k >= LAG))
+        def _():
+            swap(k - LAG)
+
+        @pl.when(lax.rem(k, 2 * SPLIT) == 2 * SPLIT - 1)
+        def _():
+            local_tile(k // (2 * SPLIT))
 
         return c
 
+    def extra(j):
+        each(e_row(j), e_recv, j, e_send, (x, zp, t), False)
+
+    def swap(j):
+        extra(j)
+        each(e_row(j), e_recv, j, e_send, (x, zp, t), True)
+
     lax.fori_loop(0, NE, first, 0)
-
-    def extra(j, c):
-        each(e_row(j), e_recv, j, e_send, (x, zp, t), False)
-
-        @pl.when(middle == 1)
-        def _():
-            each(e_row(j), e_recv, j, e_send, (x, zp, t), True)
-
-        @pl.when(NE // 2 + j < n_local)
-        def _():
-            local_tile(NE // 2 + j)
-
-        return c
-
-    lax.fori_loop(0, NE, extra, 0)
+    lax.fori_loop(NE - middle * LAG, NE, lambda j, c: (swap(j), c)[1], 0)
+    lax.fori_loop(NE // (2 * SPLIT), n_local, lambda i, c: (local_tile(i), c)[1], 0)
     w_y.wait_recv()
     w_x.start()
     w_d0.start()
@@ -217,31 +216,40 @@
     w_d1_in.wait_recv()
 
     def third(i, c):
-        step(CATCH + 2 * i)
+        for s in range(SPLIT):
+            step(CATCH + 2 * SPLIT * i + s)
 
         @pl.when(i == 0)
         def _():
+            lax.fori_loop(middle * NE, NE, lambda j, c: (extra(j), c)[1], 0)
             lax.fori_loop(0, NE // cpt, lambda j, d: (tile(e_row(cpt * j)), d)[1], 0)
 
         y_tile(i)
-        step(CATCH + 2 * i + 1)
-        z_tile(i)
+        for s in range(SPLIT):
+            step(CATCH + 2 * SPLIT * i + SPLIT + s)
+
+        @pl.when(i < CAUGHT - 1)
+        def _():
+            z_tile(i)
+
         return c
 
     lax.fori_loop(0, CAUGHT, third, 0)
 
     def steps(lo, hi):
-        lax.fori_loop(jnp.maximum(lo, CATCH + 2 * CAUGHT), jnp.minimum(hi, NY), lambda k, c: (step(k), c)[1], 0)
+        lax.fori_loop(jnp.maximum(lo, CATCH + 2 * SPLIT * CAUGHT), jnp.minimum(hi, NY), lambda k, c: (step(k), c)[1], 0)
 
     def fourth(i, c):
         steps(cpt * i + 1, cpt * i + cpt)
         y_tile(i)
         steps(cpt * i + cpt, cpt * i + cpt + 1)
-        z_tile(i)
+        z_tile(i - 1)
         return c
 
     lax.fori_loop(CAUGHT, NR // cpt, fourth, 0)
-    steps(NR + 1, NY)
+    steps(NR + 1, NY - 1)
+    z_tile(NR // cpt - 1)
+    steps(NY - 1, NY)
 
     def share(src, dst, send, recv):
         for d in range(1, 4):

time: 271 us -> 269 us (level)
  no operation moved by 1% of the time
where the time goes in v3:
time: 269 us
  Pallas kernels  268 us (100%)
    pallas_call x1, Pallas kernels, local_step(): pl.pallas_call(gather_matmul, out_shape=(pltpu.VMEM((rows, width), F32),...  260 us
    pallas_call x1, Pallas kernels, local_step(): pl.pallas_call(functools.partial(normalize, width * col_groups), out_shap...  7.82 us

profile of v3, /device:TPU:0, one launch (start us, length us, event | category | flops | bytes accessed | tf_op | source)
XLA Modules:
  0.0 268.7 jit_solution(6643081187348871155)
XLA Ops:
  0.6 0.0 copy-start
  0.6 260.3 %gather_matmul.1 = (f32[4096,1280]{1,0:T(8,128)S(1)}, f32[32,128]{1,0:T(8,128)S(1)}, bf16[4096,1280]{1,0:T(8,128)(2,1)}) custom-call(bf16[16384,1280]{1,0:T(8,128)(2,1)} %a.1, bf16[1280,1280]{1,0:T(8,128)(2,1)} %w.1, bf16[4096,1280]{1,0:T(8,128)(2,1)} %res.1), custom_call_target="tpu_custom_call" | custom-call | flops 53687091200 | bytes 41943040 | tf_op jit(solution)/shard_map/gather_matmul/pallas_call | solution.py:343
  260.9 0.0 copy-done
  260.9 7.8 %normalize.1 = (bf16[4096,1280]{1,0:T(8,128)(2,1)}, bf16[4096,1280]{1,0:T(8,128)(2,1)}) custom-call(f32[4096,1280]{1,0:T(8,128)S(1)} %get-tuple-element.4.h, f32[32,128]{1,0:T(8,128)S(1)} %get-tuple-element.5.ss, f32[1280]{0:T(1024)S(1)} %copy-done), custom_call_target="tpu_custom_call" | custom-call | tf_op jit(solution)/shard_map/normalize/pallas_call | solution.py:360
Async XLA Ops:
  0.6 260.3 %copy-start = (f32[1280]{0:T(1024)S(1)}, f32[1280]{0:T(1024)}, u32[]{:S(2)}) copy-start(f32[1280]{0:T(1024)} %gain.1) | copy-start | bytes 15364

commit v4 on v3

--- a/solution.py
+++ b/solution.py
@@ -14,7 +14,7 @@
 SPLIT = 1
 NCH, NU, NY, NR, NE = 128 * SPLIT, 60 * SPLIT, 60 * SPLIT, 56 * SPLIT, 12 * SPLIT
 LOOK, LAG = 6 * SPLIT, 3
-CATCH, CAUGHT = 24 * SPLIT, 10
+CATCH, CAUGHT, AHEAD = 24 * SPLIT, 10, 4
 TILE = 128
 LOCAL = 256
 STORE = 128
@@ -114,6 +114,10 @@
         for c in loads(i):
             c.wait()
 
+        @pl.when(i + AHEAD < n_local)
+        def _():
+            sib_copy(i + AHEAD).start()
+
         @pl.when(i + 1 < n_local)
         def _():
             prefetch(i + 1)
@@ -143,9 +147,12 @@
     def y_tile(i):
         tile(y_row(z, cpt * i))
 
-    def z_tile(i):
+    def z_wait(i):
         for s in range(cpt):
             wait_z(cpt * i + s)
+
+    def z_tile(i):
+        z_wait(i)
         tile(y_row(zp, cpt * i))
 
     barrier = pltpu.get_barrier_semaphore()
@@ -154,12 +161,14 @@
         pl.semaphore_signal(barrier, inc=1, device_id=dev, device_id_type=MESH)
     pl.semaphore_wait(barrier, len(partners))
 
+    ss_own[...] = jnp.zeros_like(ss_own)
     for k in range(LOOK):
         start_y(k)
     own = pltpu.make_async_copy(w, wbuf.at[pl.ds(0, depth)], own_w)
     own.start()
     w_sib.start()
-    lax.fori_loop(0, n_local, lambda i, c: (sib_copy(i).start(), c)[1], 0)
+    for i in range(AHEAD):
+        sib_copy(i).start()
     prefetch(0)
     own.wait()
     w_sib.wait_recv()
@@ -247,10 +256,6 @@
         return c
 
     lax.fori_loop(CAUGHT, NR // cpt, fourth, 0)
-    steps(NR + 1, NY - 1)
-    z_tile(NR // cpt - 1)
-    steps(NY - 1, NY)
-
     def share(src, dst, send, recv):
         for d in range(1, 4):
             pltpu.make_async_remote_copy(src_ref=src, dst_ref=dst.at[z], send_sem=send.at[d], recv_sem=recv.at[z],
@@ -265,7 +270,15 @@
         return (dst[0] + dst[1]) + (dst[2] + dst[3])
 
     share(ss_own, ss_all, ss_send, ss_recv)
-    ss_last[...] = jnp.broadcast_to(remote_tile(NR * ch), ss_last.shape)
+    steps(NR + 1, NY)
+
+    n_pair = NR // cpt - 1
+    in_first, in_second = n_pair, NU // cpt + n_pair
+    ss_last[...] = jnp.zeros_like(ss_last)
+    ss_last[pl.ds(0, 1), :] = remote_tile(NR * ch)
+    ss_last[pl.ds(1 + middle, 1), :] = ss_own[pl.ds(y_row(z, n_pair * cpt) // TILE, 1), :]
+    z_wait(n_pair)
+    ss_last[pl.ds(2 - middle, 1), :] = remote_tile(y_row(zp, n_pair * cpt))
     share(ss_last, ss_lasts, sl_send, sl_recv)
     y_total = 2 * NY * ch
     pltpu.make_async_remote_copy(src_ref=a.at[pl.ds(0, y_total)], dst_ref=arem.at[pl.ds(0, y_total)], send_sem=y_send, recv_sem=y_recv.at[0, 0],
@@ -285,7 +298,9 @@
     for c in (w_sib, w_y, w_x, w_d0, w_d1):
         c.wait_send()
     ss_out[...] = collect(ss_own, ss_all, ss_send, ss_recv)
-    ss_out[pl.ds(NR * ch // TILE, 1), :] = collect(ss_last, ss_lasts, sl_send, sl_recv)[:1]
+    last = collect(ss_last, ss_lasts, sl_send, sl_recv)
+    for j, row in enumerate((NR * ch // TILE, in_first, in_second)):
+        ss_out[pl.ds(row, 1), :] = last[j:j + 1]
 
 
 def normalize(total_cols, h, ss, gain, h_hbm, n_hbm, h_out, n_out, sem):

time: 269 us -> 269 us (level)
  no operation moved by 1% of the time
where the time goes in v4:
time: 269 us
  Pallas kernels  268 us (100%)
    pallas_call x1, Pallas kernels, local_step(): pl.pallas_call(gather_matmul, out_shape=(pltpu.VMEM((rows, width), F32),...  260 us
    pallas_call x1, Pallas kernels, local_step(): pl.pallas_call(functools.partial(normalize, width * col_groups), out_shap...  7.82 us

profile of v4, /device:TPU:0, one launch (start us, length us, event | category | flops | bytes accessed | tf_op | source)
XLA Modules:
  0.0 268.6 jit_solution(13640806442476438645)
XLA Ops:
  0.6 0.0 copy-start
  0.6 260.2 %gather_matmul.1 = (f32[4096,1280]{1,0:T(8,128)S(1)}, f32[32,128]{1,0:T(8,128)S(1)}, bf16[4096,1280]{1,0:T(8,128)(2,1)}) custom-call(bf16[16384,1280]{1,0:T(8,128)(2,1)} %a.1, bf16[1280,1280]{1,0:T(8,128)(2,1)} %w.1, bf16[4096,1280]{1,0:T(8,128)(2,1)} %res.1), custom_call_target="tpu_custom_call" | custom-call | flops 53687091200 | bytes 41943040 | tf_op jit(solution)/shard_map/gather_matmul/pallas_call | solution.py:358
  260.8 0.0 copy-done
  260.8 7.8 %normalize.1 = (bf16[4096,1280]{1,0:T(8,128)(2,1)}, bf16[4096,1280]{1,0:T(8,128)(2,1)}) custom-call(f32[4096,1280]{1,0:T(8,128)S(1)} %get-tuple-element.4.h, f32[32,128]{1,0:T(8,128)S(1)} %get-tuple-element.5.ss, f32[1280]{0:T(1024)S(1)} %copy-done), custom_call_target="tpu_custom_call" | custom-call | tf_op jit(solution)/shard_map/normalize/pallas_call | solution.py:375
Async XLA Ops:
  0.6 260.2 %copy-start = (f32[1280]{0:T(1024)S(1)}, f32[1280]{0:T(1024)}, u32[]{:S(2)}) copy-start(f32[1280]{0:T(1024)} %gain.1) | copy-start | bytes 15364
